TPU v7x, 32 devices: a whole 2x2x4 slice. The times are simulated.
32 devices in a mesh: member: 2 (over x), lon: 8 (over z, y), lat: 2 (over core).
Axes of the slice: x: 2, y: 2, z: 4, core: 2. Of those that a mesh axis runs over, the one named last changes fastest.
Arguments:
- strain_rate: float32 [3, 256, 2160], P(None, 'lon', 'lat'), may hold values from -6 to 6
- stress_start: float32 [3, 256, 2160], P(None, 'lon', 'lat'), may hold values from -3 to 3
- concentration: float32 [256, 2160], P('lon', 'lat'), may hold values from 0.5 to 1
- cell_class: int32 [512, 2160], P(('member', 'lon'), 'lat'), parts along dimension 0, may hold values from 0 to 7
- land_mask: int32 [256, 2160], P('lon', 'lat'), may hold values 0 or 1
- fold_partner: int32 [256], replicated, may hold values from 0 to 255, each once
- kernel_weights: float32 [7, 7], replicated, may hold values from 0.05 to 0.5
Outputs:
- stress_out: float32 [3, 512, 2160], P(None, ('member', 'lon'), 'lat'), parts along dimension 1
- damage_out: float32 [512, 2160], P(('member', 'lon'), 'lat'), parts along dimension 0
- mean_overstress: float32 [6], P('member'), parts along dimension 0
There are 2 independent parts, one for each index of `member`. A program takes and returns all parts, laid end to end along the dimension named above; an argument that names none is the same for every part. Nothing has to cross between parts.
Inputs may be any that keep to these rules, and one draw needn't show every extreme that they name: `fold_partner`: each of the 256 longitude indices appears once.
All inputs are finite; a program needn't handle non-finite values. No bound on the sum of `land_mask` on one device may be relied on, other than what follows from the above.
Results may differ from a plain program's by a relative error of at most 0.0001.
Values sent between devices are 32-bit elements; how exact they have to be, the bound alone decides.
A program may use at most 64 MiB of HBM per device.

v0:
```python
import jax
import jax.numpy as jnp
from jax import lax
from jax.sharding import PartitionSpec as P

ITERS = 3


def padded_2(array, sides, width):
    for axis, dim in sides:
        size, length = (lax.axis_size(axis), array.shape[dim])
        up = [(i, (i + 1) % size) for i in range(size)]
        down = [(j, i) for i, j in up]
        last = lax.slice_in_dim(array, length - width, length, axis=dim)
        first = lax.slice_in_dim(array, 0, width, axis=dim)
        before = lax.ppermute(last, axis, up)
        after = lax.ppermute(first, axis, down)
        array = jnp.concatenate([before, array, after], axis=dim)
    return array


def smooth(padded, weights, ncols, nrows):
    side = weights.shape[0]
    total = jnp.zeros((padded.shape[0], ncols, nrows), jnp.float32)
    for first in range(side):
        for second in range(side):
            total = (
                total
                + weights[first, second] * padded[:, first : first + ncols, second : second + nrows]
            )
    return total


def extend(fields, partner, width):
    ncols = fields.shape[1]
    top = jnp.swapaxes(fields[:, :, -width:], 1, 2)
    whole_top = lax.all_gather(top, "lon", axis=2, tiled=True)
    total_cols = whole_top.shape[2]
    first_col = lax.axis_index("lon") * ncols
    columns = (first_col - width + jnp.arange(ncols + 2 * width, dtype=jnp.int32)) % total_cols
    picked = jnp.take(partner, columns)
    rows = jnp.take(whole_top, picked, axis=2)
    north = jnp.swapaxes(rows[:, ::-1, :], 1, 2)
    lat_place = lax.axis_index("lat")
    lat_last = lax.axis_size("lat") - 1
    padded = padded_2(fields, (("lon", 1), ("lat", 2)), width)
    south_rim = jnp.where(
        lat_place == 0, jnp.zeros_like(padded[:, :, :width]), padded[:, :, :width]
    )
    north_rim = jnp.where(lat_place == lat_last, north, padded[:, :, -width:])
    return jnp.concatenate([south_rim, padded[:, :, width:-width], north_rim], axis=2)


def ocean_excess(local_excess, count):
    excess, ocean_total = lax.psum((local_excess, count), ("lon", "lat"))
    return excess / (ocean_total + 1.0)


def shards(
    strain_rate, stress_start, concentration, cell_class, land_mask, fold_partner, kernel_weights
):
    width = kernel_weights.shape[0] // 2
    ocean = land_mask.astype(jnp.float32)
    ncols, nrows = ocean.shape
    denom = smooth(extend(ocean[None], fold_partner, width), kernel_weights, ncols, nrows)[0] + 1.0
    count = jnp.sum(ocean)
    damage = ocean * 0.1 * cell_class.astype(jnp.float32) * concentration
    stress = ocean[None] * stress_start
    base = concentration * jnp.exp(-2.0 * (1.0 - concentration))
    e_one, e_two, e_shear = (strain_rate[0], strain_rate[1], strain_rate[2])
    load = jnp.stack([e_one + e_two / 3.0, e_two + e_one / 3.0, e_shear / (4.0 / 3.0)]) / (
        8.0 / 9.0
    )
    means = []
    for step in range(ITERS):
        keep = 1.0 - damage
        theta = 0.5 / (keep * keep)
        elastic = ocean[None] * (stress + (base * keep)[None] * load) / (1.0 + theta)[None]
        half_diff = (elastic[0] - elastic[1]) / 2.0
        tau = jnp.sqrt(half_diff * half_diff + elastic[2] * elastic[2] + 0.25)
        ratio = (tau + 0.7 * (elastic[0] + elastic[1]) / 2.0) / (0.6 * concentration)
        over = jnp.maximum(ratio, 1.0)
        q_part = 1.0 - 1.0 / over
        local_excess = jnp.sum(ocean * (over - 1.0))
        mean_now = ocean_excess(local_excess, count)
        factor = 1.0 / (1.0 + 2.0 * mean_now)
        local_damage = ocean * (damage + factor * keep * q_part)
        local_stress = elastic * (1.0 - factor * q_part)[None]
        fields = jnp.concatenate([local_damage[None], local_stress], axis=0)
        averaged = (
            smooth(extend(fields, fold_partner, width), kernel_weights, ncols, nrows) / denom[None]
        )
        fresh = ocean[None] * (0.5 * fields + 0.5 * averaged)
        means.append(mean_now)
        damage = fresh[0]
        stress = fresh[1:]
    return (stress, damage, jnp.stack(means))


def solution(mesh):
    in_specs = (
        P(None, "lon", "lat"),
        P(None, "lon", "lat"),
        P("lon", "lat"),
        P(("member", "lon"), "lat"),
        P("lon", "lat"),
        P(),
        P(),
    )
    out_specs = (P(None, ("member", "lon"), "lat"), P(("member", "lon"), "lat"), P("member"))
    return jax.shard_map(shards, mesh=mesh, in_specs=in_specs, out_specs=out_specs, check_vma=False)
```

profile of v0, /device:TPU:0, one launch (start us, length us, event | category | flops | bytes accessed | tf_op | source)
XLA Modules:
  0.0 402.8 jit_solution(4473305265631229765)
XLA Ops:
  0.7 1.0 convert_bitcast_fusion
  1.7 3.0 collective-permute-start.4
  4.7 3.1 collective-permute-start.5
  8.0 0.9 copy-done.3
  9.0 0.7 convert_reduce_fusion
  9.8 30.9 %all-reduce = (f32[]{:T(128)}, f32[]{:T(128)}) all-reduce(f32[]{:T(128)} %get-tuple-element.12, f32[]{:T(128)} %get-tuple-element.11), channel_id=1, replica_groups=mesh['member'=2,'lon'=8,'lat'=2] {'lon','lat'}, use_global_device_ids=true, to_apply=%region_1.2 | all-reduce | flops 2 | bytes 16 | tf_op jit(solution)/shard_map/psum | solution.py:55
  42.3 4.7 %collective-permute-start.1 = (f32[4,3,1080]{2,1,0:T(4,128)S(1)}, f32[4,3,1080]{2,1,0:T(4,128)S(1)}, u32[]{:S(2)}, u32[]{:S(2)}) collective-permute-start(f32[4,3,1080]{2,1,0:T(4,128)S(1)} %get-tuple-element.45), channel_id=1, source_target_pairs={{2,0},{4,2},{6,4},{8,6},{10,8},{12,10},{14,12},{0,14},{3,1},{5,3},... | collective-permute-start | bytes 155528 | tf_op jit(solution)/shard_map/ppermute | solution.py:17
  47.0 0.7 fusion.262
  47.8 0.7 fusion.263
  48.7 0.8 gather_fusion.1
  49.5 30.5 %all_gather.13 = f32[1,3,256]{1,2,0:T(8,128)S(1)} all-gather(f32[1,3,32]{1,2,0:T(8,128)S(1)} %slice_bitcast_fusion.1), channel_id=1, replica_groups=mesh['member'=2,'lon'=8,'lat'=2] {'lon'}, dimensions={2}, use_global_device_ids=true | all-gather | bytes 3456 | tf_op jit(solution)/shard_map/all_gather | solution.py:37
  80.1 31.2 %all_gather.12 = f32[4,3,256]{1,0,2:T(4,128)S(1)} all-gather(f32[4,3,32]{1,0,2:T(4,128)S(1)} %copy.60), channel_id=1, replica_groups=mesh['member'=2,'lon'=8,'lat'=2] {'lon'}, dimensions={2}, use_global_device_ids=true | all-gather | bytes 13824 | tf_op jit(solution)/shard_map/all_gather | solution.py:37
  111.3 0.6 gather_fusion
  111.8 0.6 gather_fusion.2
  112.6 0.7 fusion.264
  113.6 0.6 collective-permute-start.7
  114.1 0.5 collective-permute-done.6
  114.6 0.4 collective-permute-done.7
  115.1 31.9 %fusion.171 = f32[32,1080]{1,0:T(8,128)S(1)} fusion(f32[1,32,1080]{2,1,0:T(8,128)S(1)} %get-tuple-element.61, f32[1,3,1080]{2,1,0:T(4,128)S(1)} %collective-permute-done.5, f32[1,3,1080]{2,1,0:T(4,128)S(1)} %collective-permute-done.4, f32[1,38,1083]{2,1,0:T(8,128)S(1)} %get-tuple-element.52, f32[1,38,1083]{2,1,0:T(8,128)S(1)} %get-tuple-element.51, ...), kind=kLoop, calls=%fused_computation.370 | loop fusion | flops 3628800 | bytes 6246916 | tf_op jit(solution)/shard_map/div | solution.py:91
  147.2 0.4 collective-permute-start.2
  147.6 0.2 collective-permute-start.3
  147.8 0.7 collective-permute-done.2
  148.5 0.3 collective-permute-done.3
  148.9 0.4 maximum_maximum_fusion
  149.2 36.4 %fusion.105 = f32[4,32,1080]{2,1,0:T(8,128)S(1)} fusion(f32[4,38,1083]{2,1,0:T(8,128)S(1)} %get-tuple-element.31, f32[4,35,1080]{2,1,0:T(8,128)S(1)} %get-tuple-element.43, f32[4,38,1083]{2,1,0:T(8,128)S(1)} %get-tuple-element.30, f32[4,35,1080]{2,1,0:T(8,128)S(1)} %get-tuple-element.42, f32[3,32,1080]{2,1,0:T(8,128)S(1)} %broadcast_multiply_fusion.2, ...), kind=kLoop, calls=%fused_computation.240 | loop fusion | flops 13962240 | bytes 27924676 | tf_op jit(solution)/shard_map/mul | solution.py:93
  185.8 0.7 multiply_reduce_fusion.1
  186.5 30.3 %psum.36 = f32[]{:T(128)} all-reduce(f32[]{:T(128)} %get-tuple-element.17), channel_id=1, replica_groups=mesh['member'=2,'lon'=8,'lat'=2] {'lon','lat'}, use_global_device_ids=true, to_apply=%region_5.8 | all-reduce | flops 1 | bytes 8 | tf_op jit(solution)/shard_map/psum | solution.py:55
  217.9 4.7 %collective-permute-start.9 = (f32[4,3,1080]{2,1,0:T(4,128)S(1)}, f32[4,3,1080]{2,1,0:T(4,128)S(1)}, u32[]{:S(2)}, u32[]{:S(2)}) collective-permute-start(f32[4,3,1080]{2,1,0:T(4,128)S(1)} %get-tuple-element.41), channel_id=1, source_target_pairs={{2,0},{4,2},{6,4},{8,6},{10,8},{12,10},{14,12},{0,14},{3,1},{5,3},... | collective-permute-start | bytes 155528 | tf_op jit(solution)/shard_map/ppermute | solution.py:17
  222.6 31.4 %all_gather.14 = f32[4,3,256]{1,0,2:T(4,128)S(1)} all-gather(f32[4,3,32]{1,0,2:T(4,128)S(1)} %copy.64), channel_id=1, replica_groups=mesh['member'=2,'lon'=8,'lat'=2] {'lon'}, dimensions={2}, use_global_device_ids=true | all-gather | bytes 13824 | tf_op jit(solution)/shard_map/all_gather | solution.py:37
  254.0 0.6 gather_fusion.3
  255.0 0.5 collective-permute-start.11
  255.6 0.7 collective-permute-done.10
  256.3 0.1 collective-permute-done.11
  256.4 0.4 maximum_maximum_fusion.2
  256.8 36.4 %fusion.54 = f32[4,32,1080]{2,1,0:T(8,128)S(1)} fusion(f32[4,38,1083]{2,1,0:T(8,128)S(1)} %get-tuple-element.27, f32[4,35,1080]{2,1,0:T(8,128)S(1)} %get-tuple-element.39, f32[4,38,1083]{2,1,0:T(8,128)S(1)} %get-tuple-element.26, f32[4,35,1080]{2,1,0:T(8,128)S(1)} %get-tuple-element.38, f32[3,32,1080]{2,1,0:T(8,128)S(1)} %broadcast_multiply_fusion.1, ...), kind=kLoop, calls=%fused_computation.141 | loop fusion | flops 13962240 | bytes 27924676 | tf_op jit(solution)/shard_map/mul | solution.py:93
  293.3 0.7 multiply_reduce_fusion
  294.1 30.4 %psum.37 = f32[]{:T(128)} all-reduce(f32[]{:T(128)} %get-tuple-element.15), channel_id=1, replica_groups=mesh['member'=2,'lon'=8,'lat'=2] {'lon','lat'}, use_global_device_ids=true, to_apply=%region_7.10 | all-reduce | flops 1 | bytes 8 | tf_op jit(solution)/shard_map/psum | solution.py:55
  325.6 4.7 %collective-permute-start.13 = (f32[4,3,1080]{2,1,0:T(4,128)S(1)}, f32[4,3,1080]{2,1,0:T(4,128)S(1)}, u32[]{:S(2)}, u32[]{:S(2)}) collective-permute-start(f32[4,3,1080]{2,1,0:T(4,128)S(1)} %get-tuple-element.37), channel_id=1, source_target_pairs={{2,0},{4,2},{6,4},{8,6},{10,8},{12,10},{14,12},{0,14},{3,1},{5,3},... | collective-permute-start | bytes 155528 | tf_op jit(solution)/shard_map/ppermute | solution.py:17
  330.3 31.2 %all_gather.15 = f32[4,3,256]{1,0,2:T(4,128)S(1)} all-gather(f32[4,3,32]{1,0,2:T(4,128)S(1)} %copy.66), channel_id=1, replica_groups=mesh['member'=2,'lon'=8,'lat'=2] {'lon'}, dimensions={2}, use_global_device_ids=true | all-gather | bytes 13824 | tf_op jit(solution)/shard_map/all_gather | solution.py:37
  361.5 0.6 gather_fusion.4
  362.2 0.6 pad_maximum_fusion.28
  363.1 0.5 collective-permute-start.15
  363.7 0.7 collective-permute-done.14
  364.4 0.1 collective-permute-done.15
  364.5 0.4 maximum_maximum_fusion.4
  364.9 36.4 %fusion.3 = f32[4,32,1080]{2,1,0:T(8,128)S(1)} fusion(f32[4,38,1083]{2,1,0:T(8,128)S(1)} %get-tuple-element.23, f32[4,35,1080]{2,1,0:T(8,128)S(1)} %get-tuple-element.35, f32[4,38,1083]{2,1,0:T(8,128)S(1)} %get-tuple-element.22, f32[4,35,1080]{2,1,0:T(8,128)S(1)} %get-tuple-element.34, f32[3,32,1080]{2,1,0:T(8,128)S(1)} %broadcast_multiply_fusion, ...), kind=kLoop, calls=%fused_computation.42 | loop fusion | flops 13962240 | bytes 27924676 | tf_op jit(solution)/shard_map/mul | solution.py:93
  401.3 0.7 slice_bitcast_fusion
  402.0 0.8 slice.1702
  (81 shorter events, 3.5 us)
Async XLA Ops:
  0.6 48.1 %copy-start = (s32[256]{0:T(256)S(1)}, s32[256]{0:T(256)}, u32[]{:S(2)}) copy-start(s32[256]{0:T(256)} %param.16) | copy-start | bytes 3076
  0.6 7.2 %copy-start.5 = (f32[3,32,1080]{2,1,0:T(8,128)S(1)}, f32[3,32,1080]{2,1,0:T(8,128)}, u32[]{:S(2)}) copy-start(f32[3,32,1080]{2,1,0:T(8,128)} %param.11) | copy-start | bytes 1244164
  1.7 111.6 %collective-permute-start.4 = (f32[1,3,1080]{2,1,0:T(4,128)S(1)}, f32[1,3,1080]{2,1,0:T(4,128)S(1)}, u32[]{:S(2)}, u32[]{:S(2)}) collective-permute-start(f32[1,3,1080]{2,1,0:T(4,128)S(1)} %get-tuple-element.59), channel_id=1, source_target_pairs={{0,2},{2,4},{4,6},{6,8},{8,10},{10,12},{12,14},{14,0},{1,3},{3,5},... | collective-permute-start | bytes 38888 | tf_op jit(solution)/shard_map/ppermute | solution.py:16
  4.7 3.2 copy-start.1
  4.7 3.2 copy-start.2
  4.7 3.2 copy-start.4
  4.7 108.6 %collective-permute-start.5 = (f32[1,3,1080]{2,1,0:T(4,128)S(1)}, f32[1,3,1080]{2,1,0:T(4,128)S(1)}, u32[]{:S(2)}, u32[]{:S(2)}) collective-permute-start(f32[1,3,1080]{2,1,0:T(4,128)S(1)} %get-tuple-element.60), channel_id=1, source_target_pairs={{2,0},{4,2},{6,4},{8,6},{10,8},{12,10},{14,12},{0,14},{3,1},{5,3},... | collective-permute-start | bytes 38888 | tf_op jit(solution)/shard_map/ppermute | solution.py:17
  7.9 1.0 copy-start.3
  42.3 4.8 %copy-start.6 = (f32[7,7]{1,0:T(8,128)S(1)}, f32[7,7]{1,0:T(8,128)}, u32[]{:S(2)}) copy-start(f32[7,7]{1,0:T(8,128)} %param.17) | copy-start | bytes 592
  42.3 104.8 %collective-permute-start = (f32[4,3,1080]{2,1,0:T(4,128)S(1)}, f32[4,3,1080]{2,1,0:T(4,128)S(1)}, u32[]{:S(2)}, u32[]{:S(2)}) collective-permute-start(f32[4,3,1080]{2,1,0:T(4,128)S(1)} %get-tuple-element.44), channel_id=1, source_target_pairs={{0,2},{2,4},{4,6},{6,8},{8,10},{10,12},{12,14},{14,0},{1,3},{3,5},... | collective-permute-start | bytes 155528 | tf_op jit(solution)/shard_map/ppermute | solution.py:16
  42.3 104.7 %collective-permute-start.1 = (f32[4,3,1080]{2,1,0:T(4,128)S(1)}, f32[4,3,1080]{2,1,0:T(4,128)S(1)}, u32[]{:S(2)}, u32[]{:S(2)}) collective-permute-start(f32[4,3,1080]{2,1,0:T(4,128)S(1)} %get-tuple-element.45), channel_id=1, source_target_pairs={{2,0},{4,2},{6,4},{8,6},{10,8},{12,10},{14,12},{0,14},{3,1},{5,3},... | collective-permute-start | bytes 155528 | tf_op jit(solution)/shard_map/ppermute | solution.py:17
  113.4 1.2 collective-permute-start.6
  113.6 1.4 collective-permute-start.7
  147.2 1.3 collective-permute-start.2
  147.6 1.3 collective-permute-start.3
  217.8 36.9 %collective-permute-start.8 = (f32[4,3,1080]{2,1,0:T(4,128)S(1)}, f32[4,3,1080]{2,1,0:T(4,128)S(1)}, u32[]{:S(2)}, u32[]{:S(2)}) collective-permute-start(f32[4,3,1080]{2,1,0:T(4,128)S(1)} %get-tuple-element.40), channel_id=1, source_target_pairs={{0,2},{2,4},{4,6},{6,8},{8,10},{10,12},{12,14},{14,0},{1,3},{3,5},... | collective-permute-start | bytes 155528 | tf_op jit(solution)/shard_map/ppermute | solution.py:16
  217.9 36.9 %collective-permute-start.9 = (f32[4,3,1080]{2,1,0:T(4,128)S(1)}, f32[4,3,1080]{2,1,0:T(4,128)S(1)}, u32[]{:S(2)}, u32[]{:S(2)}) collective-permute-start(f32[4,3,1080]{2,1,0:T(4,128)S(1)} %get-tuple-element.41), channel_id=1, source_target_pairs={{2,0},{4,2},{6,4},{8,6},{10,8},{12,10},{14,12},{0,14},{3,1},{5,3},... | collective-permute-start | bytes 155528 | tf_op jit(solution)/shard_map/ppermute | solution.py:17
  254.9 1.3 collective-permute-start.10
  255.0 1.4 collective-permute-start.11
  325.6 37.3 %collective-permute-start.12 = (f32[4,3,1080]{2,1,0:T(4,128)S(1)}, f32[4,3,1080]{2,1,0:T(4,128)S(1)}, u32[]{:S(2)}, u32[]{:S(2)}) collective-permute-start(f32[4,3,1080]{2,1,0:T(4,128)S(1)} %get-tuple-element.36), channel_id=1, source_target_pairs={{0,2},{2,4},{4,6},{6,8},{8,10},{10,12},{12,14},{14,0},{1,3},{3,5},... | collective-permute-start | bytes 155528 | tf_op jit(solution)/shard_map/ppermute | solution.py:16
  325.6 37.3 %collective-permute-start.13 = (f32[4,3,1080]{2,1,0:T(4,128)S(1)}, f32[4,3,1080]{2,1,0:T(4,128)S(1)}, u32[]{:S(2)}, u32[]{:S(2)}) collective-permute-start(f32[4,3,1080]{2,1,0:T(4,128)S(1)} %get-tuple-element.37), channel_id=1, source_target_pairs={{2,0},{4,2},{6,4},{8,6},{10,8},{12,10},{14,12},{0,14},{3,1},{5,3},... | collective-permute-start | bytes 155528 | tf_op jit(solution)/shard_map/ppermute | solution.py:17
  363.0 1.3 collective-permute-start.14
  363.1 1.4 collective-permute-start.15
where the time goes:
time: 405 us; the launch traced here: 403 us
  blocking collectives  216 us (53%)
  other arithmetic  148 us (37%)
  starting transfers between devices  22.8 us (6%)
  local copies, waits for them, and re-layouts  8.27 us (2%)
    all_gather x4, blocking collectives, extend(): whole_top = lax.all_gather(top, 'lon', axis=2, tiled=True)  124 us
    mul x3, other arithmetic, shards(): fresh = ocean[None] * (0.5 * fields + 0.5 * averaged)  109 us
    psum x3, blocking collectives, ocean_excess(): excess, ocean_total = lax.psum((local_excess, count), ('lon', 'lat'))  91.6 us
    div x1, other arithmetic, shards(): smooth(extend(fields, fold_partner, width), kernel_weights, ncols, nrows)  31.9 us
    ppermute x8, starting transfers between devices, padded_2(): after = lax.ppermute(first, axis, down)  19 us
  transfers between devices with their start and end apart: 16, of which 8 were waited for; matrix products, arithmetic and copies ran while one was open for 10% of the time, Pallas kernels for 0%

commit v1 on v0

--- a/solution.py
+++ b/solution.py
@@ -4,6 +4,24 @@
 from jax.sharding import PartitionSpec as P
 
 ITERS = 3
+
+
+def show_chunk(inp, axis_id="lon"):
+    heap = [inp]
+    world_n = lax.psum(1, axis_name=axis_id)
+    for q in range(world_n - 1):
+        heap.append(
+            lax.ppermute(
+                heap[-1],
+                axis_name=axis_id,
+                perm=[(to_i, (to_i + 1) % world_n) for to_i in range(world_n)],
+            )
+        )
+    return jnp.roll(
+        jnp.concatenate(heap[::-1], axis=2),
+        shift=(lax.axis_index(axis_id) + 1) * inp.shape[2],
+        axis=2,
+    )
 
 
 def padded_2(array, sides, width):
@@ -34,7 +52,7 @@
 def extend(fields, partner, width):
     ncols = fields.shape[1]
     top = jnp.swapaxes(fields[:, :, -width:], 1, 2)
-    whole_top = lax.all_gather(top, "lon", axis=2, tiled=True)
+    whole_top = show_chunk(top)
     total_cols = whole_top.shape[2]
     first_col = lax.axis_index("lon") * ncols
     columns = (first_col - width + jnp.arange(ncols + 2 * width, dtype=jnp.int32)) % total_cols

time: 405 us -> 435 us (1.074)
  waiting for transfers between devices: 3.48 us -> 152 us
  blocking collectives: 216 us -> 94.2 us
    ppermute x0 -> x28, waiting for transfers between devices: none -> 148 us  [show_chunk(): lax.ppermute(heap[-1], axis_name=axis_id, perm=[(to_i, (to_i + 1) % world...]
    all_gather x4 -> x0, blocking collectives: 124 us -> none  [extend(): whole_top = lax.all_gather(top, 'lon', axis=2, tiled=True)]
    ppermute x0 -> x28, starting transfers between devices: none -> 5.27 us  [show_chunk(): lax.ppermute(heap[-1], axis_name=axis_id, perm=[(to_i, (to_i + 1) % world...]
  transfers between devices with their start and end apart: 16 -> 44, of which waited for: 8 -> 33; matrix products, arithmetic and copies ran while one was open for 10% -> 10% of each run, Pallas kernels for 0% -> 0%
where the time goes in v1:
time: 435 us; the launch traced here: 433 us
  waiting for transfers between devices  152 us (35%)
  other arithmetic  149 us (34%)
  blocking collectives  94.2 us (22%)
  starting transfers between devices  22.2 us (5%)
  local copies, waits for them, and re-layouts  12.5 us (3%)
    ppermute x28, waiting for transfers between devices, show_chunk(): lax.ppermute(heap[-1], axis_name=axis_id, perm=[(to_i, (to_i + 1) % world...  148 us
    mul x3, other arithmetic, shards(): fresh = ocean[None] * (0.5 * fields + 0.5 * averaged)  109 us
    psum x3, blocking collectives, ocean_excess(): excess, ocean_total = lax.psum((local_excess, count), ('lon', 'lat'))  94.2 us
    div x1, other arithmetic, shards(): smooth(extend(fields, fold_partner, width), kernel_weights, ncols, nrows)  32 us
    ppermute x8, starting transfers between devices, padded_2(): after = lax.ppermute(first, axis, down)  14.6 us
  transfers between devices with their start and end apart: 44, of which 33 were waited for; matrix products, arithmetic and copies ran while one was open for 10% of the time, Pallas kernels for 0%

profile of v1, /device:TPU:0, one launch (start us, length us, event | category | flops | bytes accessed | tf_op | source)
XLA Modules:
  0.0 433.4 jit_solution(11765827114871954379)
XLA Ops:
  0.7 1.0 convert_bitcast_fusion
  1.7 3.0 collective-permute-start.14
  4.7 1.6 collective-permute-start.11
  6.3 3.2 collective-permute-start.12
  9.7 0.9 copy-done.3
  10.7 0.7 convert_reduce_fusion
  11.4 30.1 %all-reduce = (f32[]{:T(128)}, f32[]{:T(128)}) all-reduce(f32[]{:T(128)} %get-tuple-element.16, f32[]{:T(128)} %get-tuple-element.15), channel_id=1, replica_groups=mesh['member'=2,'lon'=8,'lat'=2] {'lon','lat'}, use_global_device_ids=true, to_apply=%region_1.2 | all-reduce | flops 2 | bytes 16 | tf_op jit(solution)/shard_map/psum | solution.py:73
  43.4 0.8 gather_fusion.1
  44.2 0.7 fusion.265
  44.9 5.6 %collective-permute-done.3 = f32[4,3,32]{1,2,0:T(8,128)S(1)} collective-permute-done((f32[4,3,32]{1,2,0:T(8,128)S(1)}, f32[4,3,32]{1,2,0:T(8,128)S(1)}, u32[]{:S(2)}, u32[]{:S(2)}) %collective-permute-start.3) | collective-permute-done | bytes 1568 | tf_op jit(solution)/shard_map/ppermute | solution.py:14
  50.5 0.7 fusion.266
  51.3 6.2 %collective-permute-done.4 = f32[4,3,32]{1,2,0:T(8,128)S(1)} collective-permute-done((f32[4,3,32]{1,2,0:T(8,128)S(1)}, f32[4,3,32]{1,2,0:T(8,128)S(1)}, u32[]{:S(2)}, u32[]{:S(2)}) %collective-permute-start.4) | collective-permute-done | bytes 1568 | tf_op jit(solution)/shard_map/ppermute | solution.py:14
  57.5 0.7 fusion.267
  58.3 6.2 %collective-permute-done.5 = f32[4,3,32]{1,2,0:T(8,128)S(1)} collective-permute-done((f32[4,3,32]{1,2,0:T(8,128)S(1)}, f32[4,3,32]{1,2,0:T(8,128)S(1)}, u32[]{:S(2)}, u32[]{:S(2)}) %collective-permute-start.5) | collective-permute-done | bytes 1568 | tf_op jit(solution)/shard_map/ppermute | solution.py:14
  64.7 6.9 %collective-permute-done.16 = f32[1,3,32]{1,2,0:T(8,128)S(1)} collective-permute-done((f32[1,3,32]{1,2,0:T(8,128)S(1)}, f32[1,3,32]{1,2,0:T(8,128)S(1)}, u32[]{:S(2)}, u32[]{:S(2)}) %collective-permute-start.16) | collective-permute-done | bytes 416 | tf_op jit(solution)/shard_map/ppermute | solution.py:14
  71.6 6.4 %collective-permute-done.17 = f32[1,3,32]{1,2,0:T(8,128)S(1)} collective-permute-done((f32[1,3,32]{1,2,0:T(8,128)S(1)}, f32[1,3,32]{1,2,0:T(8,128)S(1)}, u32[]{:S(2)}, u32[]{:S(2)}) %collective-permute-start.17) | collective-permute-done | bytes 416 | tf_op jit(solution)/shard_map/ppermute | solution.py:14
  78.2 6.3 %collective-permute-done.18 = f32[1,3,32]{1,2,0:T(8,128)S(1)} collective-permute-done((f32[1,3,32]{1,2,0:T(8,128)S(1)}, f32[1,3,32]{1,2,0:T(8,128)S(1)}, u32[]{:S(2)}, u32[]{:S(2)}) %collective-permute-start.18) | collective-permute-done | bytes 416 | tf_op jit(solution)/shard_map/ppermute | solution.py:14
  84.5 6.5 %collective-permute-done.19 = f32[1,3,32]{1,2,0:T(8,128)S(1)} collective-permute-done((f32[1,3,32]{1,2,0:T(8,128)S(1)}, f32[1,3,32]{1,2,0:T(8,128)S(1)}, u32[]{:S(2)}, u32[]{:S(2)}) %collective-permute-start.19) | collective-permute-done | bytes 416 | tf_op jit(solution)/shard_map/ppermute | solution.py:14
  91.6 5.9 %collective-permute-done.20 = f32[1,3,32]{1,2,0:T(8,128)S(1)} collective-permute-done((f32[1,3,32]{1,2,0:T(8,128)S(1)}, f32[1,3,32]{1,2,0:T(8,128)S(1)}, u32[]{:S(2)}, u32[]{:S(2)}) %collective-permute-start.20) | collective-permute-done | bytes 416 | tf_op jit(solution)/shard_map/ppermute | solution.py:14
  97.7 2.1 collective-permute-start.8
  100.6 4.1 collective-permute-done.8
  105.3 6.3 %collective-permute-done.9 = f32[4,3,32]{1,2,0:T(8,128)S(1)} collective-permute-done((f32[4,3,32]{1,2,0:T(8,128)S(1)}, f32[4,3,32]{1,2,0:T(8,128)S(1)}, u32[]{:S(2)}, u32[]{:S(2)}) %collective-permute-start.9) | collective-permute-done | bytes 1568 | tf_op jit(solution)/shard_map/ppermute | solution.py:14
  114.7 32.0 %fusion.171 = f32[32,1080]{1,0:T(8,128)S(1)} fusion(f32[1,32,1080]{2,1,0:T(8,128)S(1)} %get-tuple-element.65, f32[1,3,1080]{2,1,0:T(4,128)S(1)} %collective-permute-done.12, f32[1,3,1080]{2,1,0:T(4,128)S(1)} %collective-permute-done.11, f32[1,38,1083]{2,1,0:T(8,128)S(1)} %get-tuple-element.56, f32[1,38,1083]{2,1,0:T(8,128)S(1)} %get-tuple-element.55, ...), kind=kLoop, calls=%fused_computation.370 | loop fusion | flops 3628800 | bytes 6246916 | tf_op jit(solution)/shard_map/div | solution.py:109
  148.9 36.4 %fusion.105 = f32[4,32,1080]{2,1,0:T(8,128)S(1)} fusion(f32[4,38,1083]{2,1,0:T(8,128)S(1)} %get-tuple-element.35, f32[4,35,1080]{2,1,0:T(8,128)S(1)} %get-tuple-element.47, f32[4,38,1083]{2,1,0:T(8,128)S(1)} %get-tuple-element.34, f32[4,35,1080]{2,1,0:T(8,128)S(1)} %get-tuple-element.46, f32[3,32,1080]{2,1,0:T(8,128)S(1)} %broadcast_multiply_fusion.2, ...), kind=kLoop, calls=%fused_computation.240 | loop fusion | flops 13962240 | bytes 27924676 | tf_op jit(solution)/shard_map/mul | solution.py:111
  185.5 0.7 multiply_reduce_fusion.1
  186.2 30.3 %psum.36 = f32[]{:T(128)} all-reduce(f32[]{:T(128)} %get-tuple-element.21), channel_id=1, replica_groups=mesh['member'=2,'lon'=8,'lat'=2] {'lon','lat'}, use_global_device_ids=true, to_apply=%region_5.9 | all-reduce | flops 1 | bytes 8 | tf_op jit(solution)/shard_map/psum | solution.py:73
  217.4 6.9 %collective-permute-done.25 = f32[4,3,32]{1,2,0:T(8,128)S(1)} collective-permute-done((f32[4,3,32]{1,2,0:T(8,128)S(1)}, f32[4,3,32]{1,2,0:T(8,128)S(1)}, u32[]{:S(2)}, u32[]{:S(2)}) %collective-permute-start.25) | collective-permute-done | bytes 1568 | tf_op jit(solution)/shard_map/ppermute | solution.py:14
  224.4 7.0 %collective-permute-done.26 = f32[4,3,32]{1,2,0:T(8,128)S(1)} collective-permute-done((f32[4,3,32]{1,2,0:T(8,128)S(1)}, f32[4,3,32]{1,2,0:T(8,128)S(1)}, u32[]{:S(2)}, u32[]{:S(2)}) %collective-permute-start.26) | collective-permute-done | bytes 1568 | tf_op jit(solution)/shard_map/ppermute | solution.py:14
  231.3 7.0 %collective-permute-done.27 = f32[4,3,32]{1,2,0:T(8,128)S(1)} collective-permute-done((f32[4,3,32]{1,2,0:T(8,128)S(1)}, f32[4,3,32]{1,2,0:T(8,128)S(1)}, u32[]{:S(2)}, u32[]{:S(2)}) %collective-permute-start.27) | collective-permute-done | bytes 1568 | tf_op jit(solution)/shard_map/ppermute | solution.py:14
  238.3 7.0 %collective-permute-done.28 = f32[4,3,32]{1,2,0:T(8,128)S(1)} collective-permute-done((f32[4,3,32]{1,2,0:T(8,128)S(1)}, f32[4,3,32]{1,2,0:T(8,128)S(1)}, u32[]{:S(2)}, u32[]{:S(2)}) %collective-permute-start.28) | collective-permute-done | bytes 1568 | tf_op jit(solution)/shard_map/ppermute | solution.py:14
  245.3 7.6 %collective-permute-done.29 = f32[4,3,32]{1,2,0:T(8,128)S(1)} collective-permute-done((f32[4,3,32]{1,2,0:T(8,128)S(1)}, f32[4,3,32]{1,2,0:T(8,128)S(1)}, u32[]{:S(2)}, u32[]{:S(2)}) %collective-permute-start.29) | collective-permute-done | bytes 1568 | tf_op jit(solution)/shard_map/ppermute | solution.py:14
  252.9 7.5 %collective-permute-done.30 = f32[4,3,32]{1,2,0:T(8,128)S(1)} collective-permute-done((f32[4,3,32]{1,2,0:T(8,128)S(1)}, f32[4,3,32]{1,2,0:T(8,128)S(1)}, u32[]{:S(2)}, u32[]{:S(2)}) %collective-permute-start.30) | collective-permute-done | bytes 1568 | tf_op jit(solution)/shard_map/ppermute | solution.py:14
  260.6 4.9 %collective-permute-start.23 = (f32[4,3,1080]{2,1,0:T(4,128)S(1)}, f32[4,3,1080]{2,1,0:T(4,128)S(1)}, u32[]{:S(2)}, u32[]{:S(2)}) collective-permute-start(f32[4,3,1080]{2,1,0:T(4,128)S(1)} %get-tuple-element.45), channel_id=1, source_target_pairs={{2,0},{4,2},{6,4},{8,6},{10,8},{12,10},{14,12},{0,14},{3,1},{5,3},... | collective-permute-start | bytes 155528 | tf_op jit(solution)/shard_map/ppermute | solution.py:35
  266.1 1.3 collective-permute-done.31
  270.8 36.4 %fusion.54 = f32[4,32,1080]{2,1,0:T(8,128)S(1)} fusion(f32[4,38,1083]{2,1,0:T(8,128)S(1)} %get-tuple-element.31, f32[4,35,1080]{2,1,0:T(8,128)S(1)} %get-tuple-element.43, f32[4,38,1083]{2,1,0:T(8,128)S(1)} %get-tuple-element.30, f32[4,35,1080]{2,1,0:T(8,128)S(1)} %get-tuple-element.42, f32[3,32,1080]{2,1,0:T(8,128)S(1)} %broadcast_multiply_fusion.1, ...), kind=kLoop, calls=%fused_computation.141 | loop fusion | flops 13962240 | bytes 27924676 | tf_op jit(solution)/shard_map/mul | solution.py:111
  307.4 0.7 multiply_reduce_fusion
  308.1 33.8 %psum.37 = f32[]{:T(128)} all-reduce(f32[]{:T(128)} %get-tuple-element.19), channel_id=1, replica_groups=mesh['member'=2,'lon'=8,'lat'=2] {'lon','lat'}, use_global_device_ids=true, to_apply=%region_7.11 | all-reduce | flops 1 | bytes 8 | tf_op jit(solution)/shard_map/psum | solution.py:73
  342.9 6.9 %collective-permute-done.36 = f32[4,3,32]{1,2,0:T(8,128)S(1)} collective-permute-done((f32[4,3,32]{1,2,0:T(8,128)S(1)}, f32[4,3,32]{1,2,0:T(8,128)S(1)}, u32[]{:S(2)}, u32[]{:S(2)}) %collective-permute-start.36) | collective-permute-done | bytes 1568 | tf_op jit(solution)/shard_map/ppermute | solution.py:14
  349.9 7.5 %collective-permute-done.37 = f32[4,3,32]{1,2,0:T(8,128)S(1)} collective-permute-done((f32[4,3,32]{1,2,0:T(8,128)S(1)}, f32[4,3,32]{1,2,0:T(8,128)S(1)}, u32[]{:S(2)}, u32[]{:S(2)}) %collective-permute-start.37) | collective-permute-done | bytes 1568 | tf_op jit(solution)/shard_map/ppermute | solution.py:14
  357.4 7.0 %collective-permute-done.38 = f32[4,3,32]{1,2,0:T(8,128)S(1)} collective-permute-done((f32[4,3,32]{1,2,0:T(8,128)S(1)}, f32[4,3,32]{1,2,0:T(8,128)S(1)}, u32[]{:S(2)}, u32[]{:S(2)}) %collective-permute-start.38) | collective-permute-done | bytes 1568 | tf_op jit(solution)/shard_map/ppermute | solution.py:14
  364.3 7.0 %collective-permute-done.39 = f32[4,3,32]{1,2,0:T(8,128)S(1)} collective-permute-done((f32[4,3,32]{1,2,0:T(8,128)S(1)}, f32[4,3,32]{1,2,0:T(8,128)S(1)}, u32[]{:S(2)}, u32[]{:S(2)}) %collective-permute-start.39) | collective-permute-done | bytes 1568 | tf_op jit(solution)/shard_map/ppermute | solution.py:14
  371.3 7.0 %collective-permute-done.40 = f32[4,3,32]{1,2,0:T(8,128)S(1)} collective-permute-done((f32[4,3,32]{1,2,0:T(8,128)S(1)}, f32[4,3,32]{1,2,0:T(8,128)S(1)}, u32[]{:S(2)}, u32[]{:S(2)}) %collective-permute-start.40) | collective-permute-done | bytes 1568 | tf_op jit(solution)/shard_map/ppermute | solution.py:14
  378.3 4.8 %collective-permute-start.34 = (f32[4,3,1080]{2,1,0:T(4,128)S(1)}, f32[4,3,1080]{2,1,0:T(4,128)S(1)}, u32[]{:S(2)}, u32[]{:S(2)}) collective-permute-start(f32[4,3,1080]{2,1,0:T(4,128)S(1)} %get-tuple-element.41), channel_id=1, source_target_pairs={{2,0},{4,2},{6,4},{8,6},{10,8},{12,10},{14,12},{0,14},{3,1},{5,3},... | collective-permute-start | bytes 155528 | tf_op jit(solution)/shard_map/ppermute | solution.py:35
  383.1 2.1 collective-permute-done.41
  386.5 5.7 %collective-permute-done.42 = f32[4,3,32]{1,2,0:T(8,128)S(1)} collective-permute-done((f32[4,3,32]{1,2,0:T(8,128)S(1)}, f32[4,3,32]{1,2,0:T(8,128)S(1)}, u32[]{:S(2)}, u32[]{:S(2)}) %collective-permute-start.42) | collective-permute-done | bytes 1568 | tf_op jit(solution)/shard_map/ppermute | solution.py:14
  395.5 36.4 %fusion.3 = f32[4,32,1080]{2,1,0:T(8,128)S(1)} fusion(f32[4,38,1083]{2,1,0:T(8,128)S(1)} %get-tuple-element.27, f32[4,35,1080]{2,1,0:T(8,128)S(1)} %get-tuple-element.39, f32[4,38,1083]{2,1,0:T(8,128)S(1)} %get-tuple-element.26, f32[4,35,1080]{2,1,0:T(8,128)S(1)} %get-tuple-element.38, f32[3,32,1080]{2,1,0:T(8,128)S(1)} %broadcast_multiply_fusion, ...), kind=kLoop, calls=%fused_computation.42 | loop fusion | flops 13962240 | bytes 27924676 | tf_op jit(solution)/shard_map/mul | solution.py:111
  432.0 0.7 slice_bitcast_fusion
  432.6 0.8 slice.1702
  (174 shorter events, 18.0 us)
Async XLA Ops:
  0.6 42.7 %copy-start = (s32[256]{0:T(256)S(1)}, s32[256]{0:T(256)}, u32[]{:S(2)}) copy-start(s32[256]{0:T(256)} %param.18) | copy-start | bytes 3076
  0.6 8.9 %copy-start.5 = (f32[3,32,1080]{2,1,0:T(8,128)S(1)}, f32[3,32,1080]{2,1,0:T(8,128)}, u32[]{:S(2)}) copy-start(f32[3,32,1080]{2,1,0:T(8,128)} %param.13) | copy-start | bytes 1244164
  1.7 56.5 %collective-permute-start.14 = (f32[1,3,32]{1,2,0:T(8,128)S(1)}, f32[1,3,32]{1,2,0:T(8,128)S(1)}, u32[]{:S(2)}, u32[]{:S(2)}) collective-permute-start(f32[1,3,32]{1,2,0:T(8,128)S(1)} %slice_bitcast_fusion.1), channel_id=1, source_target_pairs={{0,2},{2,4},{4,6},{6,8},{8,10},{10,12},{12,14},{14,0},{1,3},{3,5},... | collective-permute-start | bytes 1160 | tf_op jit(solution)/shard_map/ppermute | solution.py:14
  4.7 108.1 %collective-permute-start.11 = (f32[1,3,1080]{2,1,0:T(4,128)S(1)}, f32[1,3,1080]{2,1,0:T(4,128)S(1)}, u32[]{:S(2)}, u32[]{:S(2)}) collective-permute-start(f32[1,3,1080]{2,1,0:T(4,128)S(1)} %get-tuple-element.63), channel_id=1, source_target_pairs={{0,2},{2,4},{4,6},{6,8},{8,10},{10,12},{12,14},{14,0},{1,3},{3,5},... | collective-permute-start | bytes 38888 | tf_op jit(solution)/shard_map/ppermute | solution.py:34
  6.3 3.3 copy-start.2
  6.3 3.3 copy-start.4
  6.3 106.6 %collective-permute-start.12 = (f32[1,3,1080]{2,1,0:T(4,128)S(1)}, f32[1,3,1080]{2,1,0:T(4,128)S(1)}, u32[]{:S(2)}, u32[]{:S(2)}) collective-permute-start(f32[1,3,1080]{2,1,0:T(4,128)S(1)} %get-tuple-element.64), channel_id=1, source_target_pairs={{2,0},{4,2},{6,4},{8,6},{10,8},{12,10},{14,12},{0,14},{3,1},{5,3},... | collective-permute-start | bytes 38888 | tf_op jit(solution)/shard_map/ppermute | solution.py:35
  43.2 7.4 %collective-permute-start.3 = (f32[4,3,32]{1,2,0:T(8,128)S(1)}, f32[4,3,32]{1,2,0:T(8,128)S(1)}, u32[]{:S(2)}, u32[]{:S(2)}) collective-permute-start(f32[4,3,32]{1,2,0:T(8,128)S(1)} %fusion.256), channel_id=1, source_target_pairs={{0,2},{2,4},{4,6},{6,8},{8,10},{10,12},{12,14},{14,0},{1,3},{3,5},... | collective-permute-start | bytes 4616 | tf_op jit(solution)/shard_map/ppermute | solution.py:14
  43.2 103.4 %collective-permute-start = (f32[4,3,1080]{2,1,0:T(4,128)S(1)}, f32[4,3,1080]{2,1,0:T(4,128)S(1)}, u32[]{:S(2)}, u32[]{:S(2)}) collective-permute-start(f32[4,3,1080]{2,1,0:T(4,128)S(1)} %get-tuple-element.48), channel_id=1, source_target_pairs={{0,2},{2,4},{4,6},{6,8},{8,10},{10,12},{12,14},{14,0},{1,3},{3,5},... | collective-permute-start | bytes 155528 | tf_op jit(solution)/shard_map/ppermute | solution.py:34
  50.5 7.0 %collective-permute-start.4 = (f32[4,3,32]{1,2,0:T(8,128)S(1)}, f32[4,3,32]{1,2,0:T(8,128)S(1)}, u32[]{:S(2)}, u32[]{:S(2)}) collective-permute-start(f32[4,3,32]{1,2,0:T(8,128)S(1)} %collective-permute-done.3), channel_id=1, source_target_pairs={{0,2},{2,4},{4,6},{6,8},{8,10},{10,12},{12,14},{14,0},{1,3},{3,5},... | collective-permute-start | bytes 4616 | tf_op jit(solution)/shard_map/ppermute | solution.py:14
  57.5 7.0 %collective-permute-start.5 = (f32[4,3,32]{1,2,0:T(8,128)S(1)}, f32[4,3,32]{1,2,0:T(8,128)S(1)}, u32[]{:S(2)}, u32[]{:S(2)}) collective-permute-start(f32[4,3,32]{1,2,0:T(8,128)S(1)} %collective-permute-done.4), channel_id=1, source_target_pairs={{0,2},{2,4},{4,6},{6,8},{8,10},{10,12},{12,14},{14,0},{1,3},{3,5},... | collective-permute-start | bytes 4616 | tf_op jit(solution)/shard_map/ppermute | solution.py:14
  58.2 6.5 %collective-permute-start.15 = (f32[1,3,32]{1,2,0:T(8,128)S(1)}, f32[1,3,32]{1,2,0:T(8,128)S(1)}, u32[]{:S(2)}, u32[]{:S(2)}) collective-permute-start(f32[1,3,32]{1,2,0:T(8,128)S(1)} %collective-permute-done.14), channel_id=1, source_target_pairs={{0,2},{2,4},{4,6},{6,8},{8,10},{10,12},{12,14},{14,0},{1,3},{3,5},... | collective-permute-start | bytes 1160 | tf_op jit(solution)/shard_map/ppermute | solution.py:14
  64.5 7.1 %collective-permute-start.6 = (f32[4,3,32]{1,2,0:T(8,128)S(1)}, f32[4,3,32]{1,2,0:T(8,128)S(1)}, u32[]{:S(2)}, u32[]{:S(2)}) collective-permute-start(f32[4,3,32]{1,2,0:T(8,128)S(1)} %collective-permute-done.5), channel_id=1, source_target_pairs={{0,2},{2,4},{4,6},{6,8},{8,10},{10,12},{12,14},{14,0},{1,3},{3,5},... | collective-permute-start | bytes 4616 | tf_op jit(solution)/shard_map/ppermute | solution.py:14
  64.7 6.9 %collective-permute-start.16 = (f32[1,3,32]{1,2,0:T(8,128)S(1)}, f32[1,3,32]{1,2,0:T(8,128)S(1)}, u32[]{:S(2)}, u32[]{:S(2)}) collective-permute-start(f32[1,3,32]{1,2,0:T(8,128)S(1)} %collective-permute-done.15), channel_id=1, source_target_pairs={{0,2},{2,4},{4,6},{6,8},{8,10},{10,12},{12,14},{14,0},{1,3},{3,5},... | collective-permute-start | bytes 1160 | tf_op jit(solution)/shard_map/ppermute | solution.py:14
  71.6 6.4 %collective-permute-start.17 = (f32[1,3,32]{1,2,0:T(8,128)S(1)}, f32[1,3,32]{1,2,0:T(8,128)S(1)}, u32[]{:S(2)}, u32[]{:S(2)}) collective-permute-start(f32[1,3,32]{1,2,0:T(8,128)S(1)} %collective-permute-done.16), channel_id=1, source_target_pairs={{0,2},{2,4},{4,6},{6,8},{8,10},{10,12},{12,14},{14,0},{1,3},{3,5},... | collective-permute-start | bytes 1160 | tf_op jit(solution)/shard_map/ppermute | solution.py:14
  71.6 26.1 %collective-permute-start.7 = (f32[4,3,32]{1,2,0:T(8,128)S(1)}, f32[4,3,32]{1,2,0:T(8,128)S(1)}, u32[]{:S(2)}, u32[]{:S(2)}) collective-permute-start(f32[4,3,32]{1,2,0:T(8,128)S(1)} %collective-permute-done.6), channel_id=1, source_target_pairs={{0,2},{2,4},{4,6},{6,8},{8,10},{10,12},{12,14},{14,0},{1,3},{3,5},... | collective-permute-start | bytes 4616 | tf_op jit(solution)/shard_map/ppermute | solution.py:14
  78.0 6.4 %collective-permute-start.18 = (f32[1,3,32]{1,2,0:T(8,128)S(1)}, f32[1,3,32]{1,2,0:T(8,128)S(1)}, u32[]{:S(2)}, u32[]{:S(2)}) collective-permute-start(f32[1,3,32]{1,2,0:T(8,128)S(1)} %collective-permute-done.17), channel_id=1, source_target_pairs={{0,2},{2,4},{4,6},{6,8},{8,10},{10,12},{12,14},{14,0},{1,3},{3,5},... | collective-permute-start | bytes 1160 | tf_op jit(solution)/shard_map/ppermute | solution.py:14
  84.5 6.5 %collective-permute-start.19 = (f32[1,3,32]{1,2,0:T(8,128)S(1)}, f32[1,3,32]{1,2,0:T(8,128)S(1)}, u32[]{:S(2)}, u32[]{:S(2)}) collective-permute-start(f32[1,3,32]{1,2,0:T(8,128)S(1)} %collective-permute-done.18), channel_id=1, source_target_pairs={{0,2},{2,4},{4,6},{6,8},{8,10},{10,12},{12,14},{14,0},{1,3},{3,5},... | collective-permute-start | bytes 1160 | tf_op jit(solution)/shard_map/ppermute | solution.py:14
  91.0 6.4 %collective-permute-start.20 = (f32[1,3,32]{1,2,0:T(8,128)S(1)}, f32[1,3,32]{1,2,0:T(8,128)S(1)}, u32[]{:S(2)}, u32[]{:S(2)}) collective-permute-start(f32[1,3,32]{1,2,0:T(8,128)S(1)} %collective-permute-done.19), channel_id=1, source_target_pairs={{0,2},{2,4},{4,6},{6,8},{8,10},{10,12},{12,14},{14,0},{1,3},{3,5},... | collective-permute-start | bytes 1160 | tf_op jit(solution)/shard_map/ppermute | solution.py:14
  97.4 49.2 %collective-permute-start.1 = (f32[4,3,1080]{2,1,0:T(4,128)S(1)}, f32[4,3,1080]{2,1,0:T(4,128)S(1)}, u32[]{:S(2)}, u32[]{:S(2)}) collective-permute-start(f32[4,3,1080]{2,1,0:T(4,128)S(1)} %get-tuple-element.49), channel_id=1, source_target_pairs={{2,0},{4,2},{6,4},{8,6},{10,8},{12,10},{14,12},{0,14},{3,1},{5,3},... | collective-permute-start | bytes 155528 | tf_op jit(solution)/shard_map/ppermute | solution.py:35
  97.7 7.0 %collective-permute-start.8 = (f32[4,3,32]{1,2,0:T(8,128)S(1)}, f32[4,3,32]{1,2,0:T(8,128)S(1)}, u32[]{:S(2)}, u32[]{:S(2)}) collective-permute-start(f32[4,3,32]{1,2,0:T(8,128)S(1)} %collective-permute-done.7), channel_id=1, source_target_pairs={{0,2},{2,4},{4,6},{6,8},{8,10},{10,12},{12,14},{14,0},{1,3},{3,5},... | collective-permute-start | bytes 4616 | tf_op jit(solution)/shard_map/ppermute | solution.py:14
  104.7 7.0 %collective-permute-start.9 = (f32[4,3,32]{1,2,0:T(8,128)S(1)}, f32[4,3,32]{1,2,0:T(8,128)S(1)}, u32[]{:S(2)}, u32[]{:S(2)}) collective-permute-start(f32[4,3,32]{1,2,0:T(8,128)S(1)} %collective-permute-done.8), channel_id=1, source_target_pairs={{0,2},{2,4},{4,6},{6,8},{8,10},{10,12},{12,14},{14,0},{1,3},{3,5},... | collective-permute-start | bytes 4616 | tf_op jit(solution)/shard_map/ppermute | solution.py:14
  112.9 1.2 collective-permute-start.13
  113.1 1.4 collective-permute-start.21
  146.8 1.3 collective-permute-start.2
  147.2 1.3 collective-permute-start.10
  217.4 7.0 %collective-permute-start.25 = (f32[4,3,32]{1,2,0:T(8,128)S(1)}, f32[4,3,32]{1,2,0:T(8,128)S(1)}, u32[]{:S(2)}, u32[]{:S(2)}) collective-permute-start(f32[4,3,32]{1,2,0:T(8,128)S(1)} %fusion.254), channel_id=1, source_target_pairs={{0,2},{2,4},{4,6},{6,8},{8,10},{10,12},{12,14},{14,0},{1,3},{3,5},... | collective-permute-start | bytes 4616 | tf_op jit(solution)/shard_map/ppermute | solution.py:14
  224.4 7.0 %collective-permute-start.26 = (f32[4,3,32]{1,2,0:T(8,128)S(1)}, f32[4,3,32]{1,2,0:T(8,128)S(1)}, u32[]{:S(2)}, u32[]{:S(2)}) collective-permute-start(f32[4,3,32]{1,2,0:T(8,128)S(1)} %collective-permute-done.25), channel_id=1, source_target_pairs={{0,2},{2,4},{4,6},{6,8},{8,10},{10,12},{12,14},{14,0},{1,3},{3,5},... | collective-permute-start | bytes 4616 | tf_op jit(solution)/shard_map/ppermute | solution.py:14
  231.3 7.0 %collective-permute-start.27 = (f32[4,3,32]{1,2,0:T(8,128)S(1)}, f32[4,3,32]{1,2,0:T(8,128)S(1)}, u32[]{:S(2)}, u32[]{:S(2)}) collective-permute-start(f32[4,3,32]{1,2,0:T(8,128)S(1)} %collective-permute-done.26), channel_id=1, source_target_pairs={{0,2},{2,4},{4,6},{6,8},{8,10},{10,12},{12,14},{14,0},{1,3},{3,5},... | collective-permute-start | bytes 4616 | tf_op jit(solution)/shard_map/ppermute | solution.py:14
  238.3 7.0 %collective-permute-start.28 = (f32[4,3,32]{1,2,0:T(8,128)S(1)}, f32[4,3,32]{1,2,0:T(8,128)S(1)}, u32[]{:S(2)}, u32[]{:S(2)}) collective-permute-start(f32[4,3,32]{1,2,0:T(8,128)S(1)} %collective-permute-done.27), channel_id=1, source_target_pairs={{0,2},{2,4},{4,6},{6,8},{8,10},{10,12},{12,14},{14,0},{1,3},{3,5},... | collective-permute-start | bytes 4616 | tf_op jit(solution)/shard_map/ppermute | solution.py:14
  245.3 7.6 %collective-permute-start.29 = (f32[4,3,32]{1,2,0:T(8,128)S(1)}, f32[4,3,32]{1,2,0:T(8,128)S(1)}, u32[]{:S(2)}, u32[]{:S(2)}) collective-permute-start(f32[4,3,32]{1,2,0:T(8,128)S(1)} %collective-permute-done.28), channel_id=1, source_target_pairs={{0,2},{2,4},{4,6},{6,8},{8,10},{10,12},{12,14},{14,0},{1,3},{3,5},... | collective-permute-start | bytes 4616 | tf_op jit(solution)/shard_map/ppermute | solution.py:14
  252.9 7.6 %collective-permute-start.30 = (f32[4,3,32]{1,2,0:T(8,128)S(1)}, f32[4,3,32]{1,2,0:T(8,128)S(1)}, u32[]{:S(2)}, u32[]{:S(2)}) collective-permute-start(f32[4,3,32]{1,2,0:T(8,128)S(1)} %collective-permute-done.29), channel_id=1, source_target_pairs={{0,2},{2,4},{4,6},{6,8},{8,10},{10,12},{12,14},{14,0},{1,3},{3,5},... | collective-permute-start | bytes 4616 | tf_op jit(solution)/shard_map/ppermute | solution.py:14
  260.4 7.0 %collective-permute-start.31 = (f32[4,3,32]{1,2,0:T(8,128)S(1)}, f32[4,3,32]{1,2,0:T(8,128)S(1)}, u32[]{:S(2)}, u32[]{:S(2)}) collective-permute-start(f32[4,3,32]{1,2,0:T(8,128)S(1)} %collective-permute-done.30), channel_id=1, source_target_pairs={{0,2},{2,4},{4,6},{6,8},{8,10},{10,12},{12,14},{14,0},{1,3},{3,5},... | collective-permute-start | bytes 4616 | tf_op jit(solution)/shard_map/ppermute | solution.py:14
  260.6 8.2 %collective-permute-start.22 = (f32[4,3,1080]{2,1,0:T(4,128)S(1)}, f32[4,3,1080]{2,1,0:T(4,128)S(1)}, u32[]{:S(2)}, u32[]{:S(2)}) collective-permute-start(f32[4,3,1080]{2,1,0:T(4,128)S(1)} %get-tuple-element.44), channel_id=1, source_target_pairs={{0,2},{2,4},{4,6},{6,8},{8,10},{10,12},{12,14},{14,0},{1,3},{3,5},... | collective-permute-start | bytes 155528 | tf_op jit(solution)/shard_map/ppermute | solution.py:34
  260.6 8.2 %collective-permute-start.23 = (f32[4,3,1080]{2,1,0:T(4,128)S(1)}, f32[4,3,1080]{2,1,0:T(4,128)S(1)}, u32[]{:S(2)}, u32[]{:S(2)}) collective-permute-start(f32[4,3,1080]{2,1,0:T(4,128)S(1)} %get-tuple-element.45), channel_id=1, source_target_pairs={{2,0},{4,2},{6,4},{8,6},{10,8},{12,10},{14,12},{0,14},{3,1},{5,3},... | collective-permute-start | bytes 155528 | tf_op jit(solution)/shard_map/ppermute | solution.py:35
  268.9 1.3 collective-permute-start.24
  269.0 1.4 collective-permute-start.32
  342.9 7.0 %collective-permute-start.36 = (f32[4,3,32]{1,2,0:T(8,128)S(1)}, f32[4,3,32]{1,2,0:T(8,128)S(1)}, u32[]{:S(2)}, u32[]{:S(2)}) collective-permute-start(f32[4,3,32]{1,2,0:T(8,128)S(1)} %fusion.252), channel_id=1, source_target_pairs={{0,2},{2,4},{4,6},{6,8},{8,10},{10,12},{12,14},{14,0},{1,3},{3,5},... | collective-permute-start | bytes 4616 | tf_op jit(solution)/shard_map/ppermute | solution.py:14
  349.9 7.5 %collective-permute-start.37 = (f32[4,3,32]{1,2,0:T(8,128)S(1)}, f32[4,3,32]{1,2,0:T(8,128)S(1)}, u32[]{:S(2)}, u32[]{:S(2)}) collective-permute-start(f32[4,3,32]{1,2,0:T(8,128)S(1)} %collective-permute-done.36), channel_id=1, source_target_pairs={{0,2},{2,4},{4,6},{6,8},{8,10},{10,12},{12,14},{14,0},{1,3},{3,5},... | collective-permute-start | bytes 4616 | tf_op jit(solution)/shard_map/ppermute | solution.py:14
  357.4 7.0 %collective-permute-start.38 = (f32[4,3,32]{1,2,0:T(8,128)S(1)}, f32[4,3,32]{1,2,0:T(8,128)S(1)}, u32[]{:S(2)}, u32[]{:S(2)}) collective-permute-start(f32[4,3,32]{1,2,0:T(8,128)S(1)} %collective-permute-done.37), channel_id=1, source_target_pairs={{0,2},{2,4},{4,6},{6,8},{8,10},{10,12},{12,14},{14,0},{1,3},{3,5},... | collective-permute-start | bytes 4616 | tf_op jit(solution)/shard_map/ppermute | solution.py:14
  364.3 7.0 %collective-permute-start.39 = (f32[4,3,32]{1,2,0:T(8,128)S(1)}, f32[4,3,32]{1,2,0:T(8,128)S(1)}, u32[]{:S(2)}, u32[]{:S(2)}) collective-permute-start(f32[4,3,32]{1,2,0:T(8,128)S(1)} %collective-permute-done.38), channel_id=1, source_target_pairs={{0,2},{2,4},{4,6},{6,8},{8,10},{10,12},{12,14},{14,0},{1,3},{3,5},... | collective-permute-start | bytes 4616 | tf_op jit(solution)/shard_map/ppermute | solution.py:14
  371.3 7.0 %collective-permute-start.40 = (f32[4,3,32]{1,2,0:T(8,128)S(1)}, f32[4,3,32]{1,2,0:T(8,128)S(1)}, u32[]{:S(2)}, u32[]{:S(2)}) collective-permute-start(f32[4,3,32]{1,2,0:T(8,128)S(1)} %collective-permute-done.39), channel_id=1, source_target_pairs={{0,2},{2,4},{4,6},{6,8},{8,10},{10,12},{12,14},{14,0},{1,3},{3,5},... | collective-permute-start | bytes 4616 | tf_op jit(solution)/shard_map/ppermute | solution.py:14
  378.2 7.0 %collective-permute-start.41 = (f32[4,3,32]{1,2,0:T(8,128)S(1)}, f32[4,3,32]{1,2,0:T(8,128)S(1)}, u32[]{:S(2)}, u32[]{:S(2)}) collective-permute-start(f32[4,3,32]{1,2,0:T(8,128)S(1)} %collective-permute-done.40), channel_id=1, source_target_pairs={{0,2},{2,4},{4,6},{6,8},{8,10},{10,12},{12,14},{14,0},{1,3},{3,5},... | collective-permute-start | bytes 4616 | tf_op jit(solution)/shard_map/ppermute | solution.py:14
  378.3 15.2 %collective-permute-start.33 = (f32[4,3,1080]{2,1,0:T(4,128)S(1)}, f32[4,3,1080]{2,1,0:T(4,128)S(1)}, u32[]{:S(2)}, u32[]{:S(2)}) collective-permute-start(f32[4,3,1080]{2,1,0:T(4,128)S(1)} %get-tuple-element.40), channel_id=1, source_target_pairs={{0,2},{2,4},{4,6},{6,8},{8,10},{10,12},{12,14},{14,0},{1,3},{3,5},... | collective-permute-start | bytes 155528 | tf_op jit(solution)/shard_map/ppermute | solution.py:34
  378.3 15.2 %collective-permute-start.34 = (f32[4,3,1080]{2,1,0:T(4,128)S(1)}, f32[4,3,1080]{2,1,0:T(4,128)S(1)}, u32[]{:S(2)}, u32[]{:S(2)}) collective-permute-start(f32[4,3,1080]{2,1,0:T(4,128)S(1)} %get-tuple-element.41), channel_id=1, source_target_pairs={{2,0},{4,2},{6,4},{8,6},{10,8},{12,10},{14,12},{0,14},{3,1},{5,3},... | collective-permute-start | bytes 155528 | tf_op jit(solution)/shard_map/ppermute | solution.py:35
  385.2 7.0 %collective-permute-start.42 = (f32[4,3,32]{1,2,0:T(8,128)S(1)}, f32[4,3,32]{1,2,0:T(8,128)S(1)}, u32[]{:S(2)}, u32[]{:S(2)}) collective-permute-start(f32[4,3,32]{1,2,0:T(8,128)S(1)} %collective-permute-done.41), channel_id=1, source_target_pairs={{0,2},{2,4},{4,6},{6,8},{8,10},{10,12},{12,14},{14,0},{1,3},{3,5},... | collective-permute-start | bytes 4616 | tf_op jit(solution)/shard_map/ppermute | solution.py:14
  393.6 1.3 collective-permute-start.35
  393.7 1.4 collective-permute-start.43
  (3 other events, 5.1 us)
